TPU v7x, 32 devices: a whole 2x2x4 slice. The times are simulated.
32 devices in a mesh: parts: 2 (over x), rows: 16 (over z, y, core).
Axes of the slice: x: 2, y: 2, z: 4, core: 2. Of those that a mesh axis runs over, the one named last changes fastest.
Arguments:
- feature_bin: int32 [16384, 700], P(('parts', 'rows')), parts along dimension 0, may hold values from 0 to 255
- doc_leaf: int32 [16384], P(('parts', 'rows')), parts along dimension 0, may hold values from 0 to 31
- current_score: float32 [16384], P(('parts', 'rows')), parts along dimension 0, may hold values from -8 to 8
- relevance: int32 [16384], P(('parts', 'rows')), parts along dimension 0, may hold values from 0 to 4
- doc_rank: int32 [16384], P(('parts', 'rows')), parts along dimension 0, may hold values from 0 to 255, as said below
- query_length: int32 [64], P(('parts', 'rows')), parts along dimension 0, may hold values from 10 to 256, as said below
- feature_votes: int32 [32, 32, 20], P(('parts', 'rows')), parts along dimension 0, may hold values from 0 to 699, all different within a row
- elected: int32 [64, 40], P('parts'), parts along dimension 0, may hold values from 0 to 699, all different within a row
Outputs:
- gradient: float32 [16384], P(('parts', 'rows')), parts along dimension 0
- hessian: float32 [16384], P(('parts', 'rows')), parts along dimension 0
- vote_count: int32 [64, 700], P('parts'), parts along dimension 0
- split_gain: float32 [64, 40, 256], P('parts'), parts along dimension 0
There are 2 independent parts, one for each index of `parts`. A program takes and returns all parts, laid end to end along the dimension named above; each array names one. Nothing has to cross between parts.
Inputs may be any that keep to these rules, and one draw needn't show every extreme that they name: `query_length`: query q holds slots q * 256 to (q + 1) * 256 - 1 of the document arrays; in every draw some query has exactly 256 documents. `doc_rank`: within each query the live documents hold positions 0 to query_length - 1, each once; slots that are not live hold positions from query_length to 255. `feature_votes`: the 20 votes of one device for one leaf are different features. The 40 elected features of one leaf are different.
All inputs are finite; a program needn't handle non-finite values.
Results may differ from a plain program's by a relative error of at most 0.0003.
Values sent between devices are 32-bit elements; how exact they have to be, the bound alone decides.
No kernel may reach another device: no remote copies, remote signals or barrier semaphores. Data moves between devices by JAX's collectives and lax.ppermute only.
A program may use at most 64 MiB of HBM per device.

v0:
```python
import math
import jax
import jax.numpy as jnp
from jax import lax
from jax.sharding import PartitionSpec as P

B = 256
QMAX = 256
ridge_weight = 1.0


def query_terms(scores, levels, places, length):
    positions = jnp.arange(scores.shape[0], dtype=jnp.int32)
    living = positions < length
    gains = jnp.exp2(levels.astype(jnp.float32)) - 1.0
    discount = 1.0 / jnp.log2(places.astype(jnp.float32) + 2.0)
    higher = (levels[None, :] > levels[:, None]) & living[None, :]
    earlier = (
        (levels[None, :] == levels[:, None])
        & (positions[None, :] < positions[:, None])
        & living[None, :]
    )
    ideal_place = jnp.sum((higher | earlier).astype(jnp.float32), axis=1)
    ideal = jnp.sum(jnp.where(living, gains / jnp.log2(ideal_place + 2.0), 0.0))
    scaling = 1.0 / jnp.maximum(ideal, 1.0)
    ordered = (levels[:, None] > levels[None, :]) & living[:, None] & living[None, :]
    chance = jax.nn.sigmoid(scores[None, :] - scores[:, None])
    change = (
        (gains[:, None] - gains[None, :]) * jnp.abs(discount[:, None] - discount[None, :]) * scaling
    )
    pushes = jnp.where(ordered, chance * change, 0.0)
    curves = jnp.where(ordered, chance * (1.0 - chance) * change, 0.0)
    return (
        jnp.sum(pushes, axis=0) - jnp.sum(pushes, axis=1),
        jnp.sum(curves, axis=0) + jnp.sum(curves, axis=1),
    )


def build_histogram(feature_bin, doc_leaf, gradient, hessian, elected, bins):
    leaves, picked = elected.shape
    documents = feature_bin.shape[0]
    leaf_hot = (doc_leaf[:, None] == jnp.arange(leaves, dtype=jnp.int32)[None, :]).astype(
        jnp.float32
    )
    columns = jnp.dot(
        leaf_hot, elected.astype(jnp.float32), precision=lax.Precision.HIGHEST
    ).astype(jnp.int32)
    chosen = jnp.take_along_axis(feature_bin, columns, axis=1)
    weighted = jnp.concatenate([leaf_hot * gradient[:, None], leaf_hot * hessian[:, None]], axis=1)
    block_rows = math.gcd(documents, 512)
    block_count = documents // block_rows
    bin_ids = jnp.arange(bins, dtype=jnp.int32)

    def add_block(index, total):
        onehot = (chosen[:, :, None] == bin_ids[None, None, :]).astype(jnp.float32)
        onehot = onehot.reshape(block_rows, picked * bins)
        return total + jnp.dot(weighted.T, onehot, precision=lax.Precision.HIGHEST)

    empty = jnp.zeros((2 * leaves, picked * bins), jnp.float32)
    total = lax.fori_loop(0, block_count, add_block, empty)
    return total.reshape(2, leaves, picked, bins)


def split_score(prefix, whole):
    remain = whole - prefix
    return (
        prefix[0] * prefix[0] / (prefix[1] + ridge_weight)
        + remain[0] * remain[0] / (remain[1] + ridge_weight)
        - whole[0] * whole[0] / (whole[1] + ridge_weight)
    )


def count_votes(feature_votes, features):
    hits = feature_votes[..., None] == jnp.arange(features, dtype=jnp.int32)
    return jnp.sum(hits.astype(jnp.int32), axis=(0, 2))


def on_device(
    feature_bin, doc_leaf, current_score, relevance, doc_rank, query_length, feature_votes, elected
):
    features = feature_bin.shape[1]
    all_votes = lax.all_gather(feature_votes, "rows", axis=0, tiled=True)
    vote_count = count_votes(all_votes, features)

    def one_query(items):
        return query_terms(items[0], items[1], items[2], items[3])

    gradient, hessian = lax.map(
        one_query,
        (
            current_score.reshape(-1, QMAX),
            relevance.reshape(-1, QMAX),
            doc_rank.reshape(-1, QMAX),
            query_length,
        ),
    )
    gradient = gradient.reshape(-1)
    hessian = hessian.reshape(-1)
    histogram = build_histogram(feature_bin, doc_leaf, gradient, hessian, elected, B)
    summed = lax.psum(histogram, "rows")
    prefix = jnp.cumsum(summed, axis=3)
    whole = jnp.sum(summed, axis=3, keepdims=True)
    split_gain = split_score(prefix, whole)
    return (gradient, hessian, vote_count, split_gain)


def solution(mesh):
    return jax.shard_map(
        on_device,
        mesh=mesh,
        in_specs=(
            P(("parts", "rows"), None),
            P(("parts", "rows")),
            P(("parts", "rows")),
            P(("parts", "rows")),
            P(("parts", "rows")),
            P(("parts", "rows")),
            P(("parts", "rows"), None, None),
            P("parts", None),
        ),
        out_specs=(
            P(("parts", "rows")),
            P(("parts", "rows")),
            P("parts", None),
            P("parts", None, None),
        ),
        check_vma=False,
    )
```

profile of v0, /device:TPU:0, one launch (start us, length us, event | category | flops | bytes accessed | tf_op | source)
XLA Modules:
  0.0 409.0 jit_solution(16073954382203800596)
XLA Ops:
  7.2 0.0 copy-start
  7.2 0.0 all-reduce.2.cloned.1.call-start
  7.3 0.8 reshape.169
  8.0 0.7 reshape.170
  8.7 0.7 reshape.171
  9.4 9.2 %while.18 = (s32[]{:T(128)}, f32[2,256]{1,0:T(2,128)S(1)}, f32[2,256]{1,0:T(2,128)S(1)}, s32[2,256]{1,0:T(2,128)S(1)}, s32[2]{0:T(128)}, /*index=5*/f32[2,256]{1...) while((s32[]{:T(128)}, f32[2,256]{1,0:T(2,128)S(1)}, f32[2,256]{1,0:T(2,128)S(1)}, ...), condition=%wide.region_7.8_spmd, body=%wide.region_0.7_spmd.sunk | while | flops 2035203 | bytes 32681 | solution.py:88
  9.5 1.2 dynamic_slice.34
  10.7 0.6 iota_compare_fusion.6
  11.4 0.2 convert_reduce_fusion.3
  11.6 1.3 exponential_add_fusion.5
  13.5 0.4 fusion.28
  14.1 1.2 dynamic_slice.34
  15.3 0.6 iota_compare_fusion.6
  16.0 0.2 convert_reduce_fusion.3
  16.2 1.3 exponential_add_fusion.5
  18.2 0.4 fusion.28
  18.6 0.0 copy-start.3
  18.7 0.0 copy-start.4
  18.7 1.0 bitcast_or_fusion
  19.7 0.1 copy.34
  19.8 0.2 reshape.179
  20.0 0.0 copy-done
  20.0 0.0 copy-start.5
  20.0 163.1 %gather_fusion = s32[20480]{0:T(1024)S(1)} fusion(s32[512,700]{0,1:T(8,128)S(1)} %copy-done, s32[20480]{0:T(1024)S(1)} %reshape.179), kind=kCustom, calls=%fused_computation | custom fusion | bytes 327680 | tf_op jit(solution)/shard_map/jit(take_along_axis)/gather | solution.py:48
  183.1 0.2 reshape.182
  183.3 0.1 copy.35
  183.4 0.0 copy-done.3
  183.4 0.0 copy-done.4
  183.4 0.0 copy-done.5
  183.5 3.3 bitcast_compare_fusion
  186.8 11.0 %fusion.22 = f32[2,32,40,256]{3,1,2,0:T(8,128)} fusion(f32[2,32,512,1]{2,1,3,0:T(8,128)S(1)} %bitcast.69, pred[40,256,512,1]{2,1,0,3:T(32,128)(4,1)S(1)} %bitcast.68), kind=kOutput, calls=%fused_computation.56 | convolution fusion | flops 4026531840 | bytes 7995392 | tf_op jit(solution)/shard_map/while/body/eval_jaxpr/dot_general | solution.py:57
  197.9 0.0 copy-start.2
  197.9 0.0 all-reduce.2.cloned.1.call-update
  197.9 0.7 copy-done.2
  198.6 24.5 %all_gather.3 = s32[16,32,20]{1,2,0:T(8,128)S(1)} all-gather(s32[1,32,20]{1,2,0:T(8,128)S(1)} %copy.33), channel_id=1, replica_groups=mesh['parts'=2,'rows'=16] {'rows'}, dimensions={0}, use_global_device_ids=true | all-gather | bytes 43520 | tf_op jit(solution)/shard_map/all_gather | solution.py:82
  223.1 4.4 %convert_reduce_fusion.1 = s32[32,700]{1,0:T(8,128)} fusion(s32[16,32,20]{1,2,0:T(8,128)S(1)} %all_gather.3), kind=kLoop, calls=%fused_computation.25 | loop fusion | flops 21481600 | bytes 130560 | tf_op jit(solution)/shard_map/reduce_sum | solution.py:75
  227.5 74.4 %all-reduce.2.cloned.1.call-done = f32[2,32,40,256]{3,1,2,0:T(8,128)} async-done(((f32[2,32,40,256]{3,1,2,0:T(8,128)}), f32[2,32,40,256]{3,1,2,0:T(8,128)}) %all-reduce.2.cloned.1.call-update) | async-done | bytes 2621456 | tf_op jit(solution)/shard_map/psum | solution.py:100
  302.0 2.2 reduce_sum.91
  304.1 0.1 copy.40
  304.2 4.3 %reshape.175 = f32[2,32,40,2,128]{4,3,1,2,0:T(2,128)} reshape(f32[2,32,40,256]{3,1,2,0:T(8,128)} %all-reduce.2.cloned.1.call-done) | data formatting | bytes 5242880 | tf_op jit(solution)/shard_map/reshape.2
  308.5 4.8 %copy.36 = f32[2,32,40,2,128]{4,2,3,1,0:T(8,128)} copy(f32[2,32,40,2,128]{4,3,1,2,0:T(2,128)} %reshape.175) | data formatting | bytes 5242880 | tf_op jit(solution)/shard_map/reshape.2
  313.3 69.9 %reduce-window.6 = f32[2,32,40,2,128]{4,2,3,1,0:T(8,128)} reduce-window(f32[2,32,40,2,128]{4,2,3,1,0:T(8,128)} %copy.36, f32[]{:T(128)} %constant.79.clone.1), window={size=1x1x1x1x128 pad=0_0x0_0x0_0x0_0x127_0}, to_apply=%region_10.11 | reduce-window | flops 83230720 | bytes 5242884 | tf_op jit(solution)/shard_map/reduce-window
  383.1 4.0 slice.41
  387.1 2.7 copy.37
  389.8 0.2 fusion.14
  390.0 0.1 copy.38
  390.0 0.0 copy-start.1
  390.0 2.3 broadcast_add_fusion
  392.4 0.2 copy-done.1
  392.5 2.3 bitcast_subtract_fusion
  394.8 0.2 fusion.13
  395.0 1.7 copy.39
  396.7 2.3 div.58
  399.1 0.1 copy.42
  399.1 3.1 fusion.12
  (24 shorter events, 0.3 us)
Async XLA Ops:
  7.2 12.8 %copy-start = (s32[512,700]{0,1:T(8,128)S(1)}, s32[512,700]{0,1:T(8,128)}, u32[]{:S(2)}) copy-start(s32[512,700]{0,1:T(8,128)} %param.10) | copy-start | bytes 4300804
  7.2 294.8 %all-reduce.2.cloned.1.call-start = ((), (), s32[]{:S(2)}) async-start(), calls=%async_computation | async-start | bytes 5242880 | tf_op jit(solution)/shard_map/psum | solution.py:100
  18.6 164.8 %copy-start.3 = (f32[1,2,2,128]{3,1,2,0:T(2,128)}, f32[1,2,2,128]{3,1,2,0:T(2,128)S(1)}, u32[]{:S(2)}) copy-start(f32[1,2,2,128]{3,1,2,0:T(2,128)S(1)} %copy.45) | copy-start | bytes 6148
  18.7 164.8 %copy-start.4 = (f32[1,2,2,128]{3,1,2,0:T(2,128)}, f32[1,2,2,128]{3,1,2,0:T(2,128)S(1)}, u32[]{:S(2)}) copy-start(f32[1,2,2,128]{3,1,2,0:T(2,128)S(1)} %copy.46) | copy-start | bytes 6148
  20.0 163.4 %copy-start.5 = (s32[512]{0:T(512)S(1)}, s32[512]{0:T(512)}, u32[]{:S(2)}) copy-start(s32[512]{0:T(512)} %param.11) | copy-start | bytes 6148
  197.9 0.7 copy-start.2
  390.0 2.5 copy-start.1
Sparse Core Ops, SparseCore 0:
  198.0 103.8 all-reduce.1
where the time goes:
time: 417 us; the launch traced here: 409 us
  local copies, waits for them, and re-layouts  189 us (45%)
  other arithmetic  92.9 us (22%)
  waiting for transfers between devices  74.4 us (18%)
  blocking collectives  24.5 us (6%)
  between operations  14.3 us (3%)
  matrix products  12 us (3%)
    gather x5, local copies, waits for them, and re-layouts, build_histogram(): chosen = jnp.take_along_axis(feature_bin, columns, axis=1)  164 us
    psum x1, waiting for transfers between devices, on_device(): summed = lax.psum(histogram, 'rows')  74.4 us
    another operation x5, other arithmetic  72.3 us
    all_gather x1, blocking collectives, on_device(): all_votes = lax.all_gather(feature_votes, 'rows', axis=0, tiled=True)  24.5 us
    dot_general x1, matrix products, add_block(): return total + jnp.dot(weighted.T, onehot, precision=lax.Precision.HIGHEST)  11 us
    another operation x4, local copies, waits for them, and re-layouts  9.1 us
  transfers between devices with their start and end apart: 1, of which 1 were waited for; matrix products, arithmetic and copies ran while one was open for 1% of the time, Pallas kernels for 0%

commit v1 on v0

--- a/solution.py
+++ b/solution.py
@@ -97,7 +97,9 @@
     gradient = gradient.reshape(-1)
     hessian = hessian.reshape(-1)
     histogram = build_histogram(feature_bin, doc_leaf, gradient, hessian, elected, B)
-    summed = lax.psum(histogram, "rows")
+    summed = histogram
+    for hop in (1, 2, 4, 8):
+        summed = summed + lax.ppermute(summed, "rows", [(dev, dev ^ hop) for dev in range(16)])
     prefix = jnp.cumsum(summed, axis=3)
     whole = jnp.sum(summed, axis=3, keepdims=True)
     split_gain = split_score(prefix, whole)

time: 417 us -> 552 us (1.32)
  blocking collectives: 24.5 us -> 122 us
  waiting for transfers between devices: 74.4 us -> 118 us
  between operations: 14.3 us -> 0.91 us
  starting transfers between devices: 0.04 us -> 7.95 us
    ppermute x0 -> x4, waiting for transfers between devices: none -> 118 us  [on_device(): lax.ppermute(summed, 'rows', [(dev, dev ^ hop) for dev in range(16)])]
    all_gather x1, blocking collectives: 24.5 us -> 122 us  [on_device(): all_votes = lax.all_gather(feature_votes, 'rows', axis=0, tiled=True)]
    psum x1 -> x0, waiting for transfers between devices: 74.4 us -> none  [on_device(): summed = lax.psum(histogram, 'rows')]
    ppermute x0 -> x4, starting transfers between devices: none -> 7.95 us  [on_device(): lax.ppermute(summed, 'rows', [(dev, dev ^ hop) for dev in range(16)])]
  transfers between devices with their start and end apart: 1 -> 4, of which waited for: 1 -> 3; matrix products, arithmetic and copies ran while one was open for 1% -> 1% of each run, Pallas kernels for 0% -> 0%
where the time goes in v1:
time: 552 us; the launch traced here: 544 us
  local copies, waits for them, and re-layouts  189 us (34%)
  blocking collectives  122 us (22%)
  waiting for transfers between devices  118 us (21%)
  other arithmetic  94.4 us (17%)
  matrix products  10.5 us (2%)
  starting transfers between devices  7.95 us (1%)
    gather x5, local copies, waits for them, and re-layouts, build_histogram(): chosen = jnp.take_along_axis(feature_bin, columns, axis=1)  164 us
    all_gather x1, blocking collectives, on_device(): all_votes = lax.all_gather(feature_votes, 'rows', axis=0, tiled=True)  122 us
    ppermute x4, waiting for transfers between devices, on_device(): lax.ppermute(summed, 'rows', [(dev, dev ^ hop) for dev in range(16)])  118 us
    another operation x5, other arithmetic  72.3 us
  transfers between devices with their start and end apart: 4, of which 3 were waited for; matrix products, arithmetic and copies ran while one was open for 1% of the time, Pallas kernels for 0%

profile of v1, /device:TPU:0, one launch (start us, length us, event | category | flops | bytes accessed | tf_op | source)
XLA Modules:
  0.0 544.1 jit_solution(17703792115951882165)
XLA Ops:
  0.6 0.0 copy-start
  0.7 0.8 reshape.169
  1.5 0.7 reshape.170
  2.2 0.7 reshape.171
  2.9 9.2 %while.18 = (s32[]{:T(128)}, f32[2,256]{1,0:T(2,128)S(1)}, f32[2,256]{1,0:T(2,128)S(1)}, s32[2,256]{1,0:T(2,128)S(1)}, s32[2]{0:T(128)}, /*index=5*/f32[2,256]{1...) while((s32[]{:T(128)}, f32[2,256]{1,0:T(2,128)S(1)}, f32[2,256]{1,0:T(2,128)S(1)}, ...), condition=%wide.region_7.8_spmd, body=%wide.region_0.7_spmd.sunk | while | flops 2035203 | bytes 32681 | solution.py:88
  2.9 1.2 dynamic_slice.34
  4.1 0.6 iota_compare_fusion.6
  4.8 0.2 convert_reduce_fusion.3
  5.0 1.3 exponential_add_fusion.5
  7.0 0.4 fusion.29
  7.5 1.2 dynamic_slice.34
  8.7 0.6 iota_compare_fusion.6
  9.4 0.2 convert_reduce_fusion.3
  9.6 1.3 exponential_add_fusion.5
  11.6 0.4 fusion.29
  12.1 0.0 copy-start.3
  12.1 0.0 copy-start.4
  12.1 1.0 bitcast_or_fusion
  13.1 0.1 copy.34
  13.2 0.2 reshape.179
  13.4 0.0 copy-done
  13.4 0.0 copy-start.5
  13.4 163.1 %gather_fusion = s32[20480]{0:T(1024)S(1)} fusion(s32[512,700]{0,1:T(8,128)S(1)} %copy-done, s32[20480]{0:T(1024)S(1)} %reshape.179), kind=kCustom, calls=%fused_computation | custom fusion | bytes 327680 | tf_op jit(solution)/shard_map/jit(take_along_axis)/gather | solution.py:48
  176.5 0.2 reshape.182
  176.7 0.1 copy.35
  176.8 0.0 copy-done.3
  176.9 0.0 copy-done.4
  176.9 0.0 copy-done.5
  176.9 3.3 bitcast_compare_fusion
  180.3 9.5 %fusion.23 = f32[2,32,40,256]{3,1,2,0:T(8,128)S(1)} fusion(f32[2,32,512,1]{2,1,3,0:T(8,128)S(1)} %bitcast.69, pred[40,256,512,1]{2,1,0,3:T(32,128)(4,1)S(1)} %bitcast.68), kind=kOutput, calls=%fused_computation.57 | convolution fusion | flops 4026531840 | bytes 7995392 | tf_op jit(solution)/shard_map/while/body/eval_jaxpr/dot_general | solution.py:57
  189.8 0.6 collective-permute-start
  190.3 4.5 collective-permute-done
  194.9 0.5 add.113
  195.4 2.9 collective-permute-start.1
  198.3 57.2 %collective-permute-done.1 = f32[2,32,40,256]{3,1,2,0:T(8,128)S(1)} collective-permute-done((f32[2,32,40,256]{3,1,2,0:T(8,128)S(1)}, f32[2,32,40,256]{3,1,2,0:T(8,128)S(1)}, u32[]{:S(2)}, u32[]{:S(2)}) %collective-permute-start.1) | collective-permute-done | bytes 2621472 | tf_op jit(solution)/shard_map/ppermute | solution.py:102
  255.5 0.5 add.114
  256.0 0.0 copy-start.2
  256.0 1.9 collective-permute-start.2
  257.9 56.5 %collective-permute-done.2 = f32[2,32,40,256]{3,1,2,0:T(8,128)S(1)} collective-permute-done((f32[2,32,40,256]{3,1,2,0:T(8,128)S(1)}, f32[2,32,40,256]{3,1,2,0:T(8,128)S(1)}, u32[]{:S(2)}, u32[]{:S(2)}) %collective-permute-start.2) | collective-permute-done | bytes 2621472 | tf_op jit(solution)/shard_map/ppermute | solution.py:102
  314.4 0.8 add.115
  315.2 2.6 collective-permute-start.3
  317.8 0.0 copy-done.2
  317.8 121.9 %all_gather.3 = s32[16,32,20]{1,2,0:T(8,128)S(1)} all-gather(s32[1,32,20]{1,2,0:T(8,128)S(1)} %copy.33), channel_id=1, replica_groups=mesh['parts'=2,'rows'=16] {'rows'}, dimensions={0}, use_global_device_ids=true | all-gather | bytes 43520 | tf_op jit(solution)/shard_map/all_gather | solution.py:82
  439.7 4.4 convert_reduce_fusion.1
  444.1 0.0 collective-permute-done.3
  444.1 1.9 fusion.22
  446.0 0.1 copy.40
  446.1 4.3 reshape.175
  450.3 4.8 copy.36
  455.1 69.9 %reduce-window.6 = f32[2,32,40,2,128]{4,2,3,1,0:T(8,128)} reduce-window(f32[2,32,40,2,128]{4,2,3,1,0:T(8,128)} %copy.36, f32[]{:T(128)} %constant.79.clone.1), window={size=1x1x1x1x128 pad=0_0x0_0x0_0x0_0x127_0}, to_apply=%region_9.10 | reduce-window | flops 83230720 | bytes 5242884 | tf_op jit(solution)/shard_map/reduce-window
  525.0 4.0 slice.41
  529.0 2.7 copy.37
  531.7 0.2 fusion.14
  531.8 0.1 copy.38
  531.9 0.0 copy-start.1
  531.9 2.3 broadcast_add_fusion
  534.2 0.2 copy-done.1
  534.4 2.3 bitcast_subtract_fusion
  536.7 0.2 fusion.13
  536.9 1.7 copy.39
  538.6 2.3 div.58
  540.9 0.1 copy.42
  541.0 3.1 fusion.12
  (24 shorter events, 0.3 us)
Async XLA Ops:
  0.6 12.8 %copy-start = (s32[512,700]{0,1:T(8,128)S(1)}, s32[512,700]{0,1:T(8,128)}, u32[]{:S(2)}) copy-start(s32[512,700]{0,1:T(8,128)} %param.10) | copy-start | bytes 4300804
  12.1 164.8 %copy-start.3 = (f32[1,2,2,128]{3,1,2,0:T(2,128)}, f32[1,2,2,128]{3,1,2,0:T(2,128)S(1)}, u32[]{:S(2)}) copy-start(f32[1,2,2,128]{3,1,2,0:T(2,128)S(1)} %copy.45) | copy-start | bytes 6148
  12.1 164.8 %copy-start.4 = (f32[1,2,2,128]{3,1,2,0:T(2,128)}, f32[1,2,2,128]{3,1,2,0:T(2,128)S(1)}, u32[]{:S(2)}) copy-start(f32[1,2,2,128]{3,1,2,0:T(2,128)S(1)} %copy.46) | copy-start | bytes 6148
  13.4 163.4 %copy-start.5 = (s32[512]{0:T(512)S(1)}, s32[512]{0:T(512)}, u32[]{:S(2)}) copy-start(s32[512]{0:T(512)} %param.11) | copy-start | bytes 6148
  189.8 5.1 collective-permute-start
  195.4 60.1 %collective-permute-start.1 = (f32[2,32,40,256]{3,1,2,0:T(8,128)S(1)}, f32[2,32,40,256]{3,1,2,0:T(8,128)S(1)}, u32[]{:S(2)}, u32[]{:S(2)}) collective-permute-start(f32[2,32,40,256]{3,1,2,0:T(8,128)S(1)} %add.113), channel_id=1, source_target_pairs={{0,2},{1,3},{2,0},{3,1},{4,6},{5,7},{6,4},{7,5},{8,10},{9,11},{10,... | collective-permute-start | bytes 7864328 | tf_op jit(solution)/shard_map/ppermute | solution.py:102
  256.0 61.8 %copy-start.2 = (s32[1,32,20]{1,0,2:T(1,128)S(1)}, s32[1,32,20]{1,0,2:T(1,128)}, u32[]{:S(2)}) copy-start(s32[1,32,20]{1,0,2:T(1,128)} %param.16) | copy-start | bytes 7684
  256.0 58.4 %collective-permute-start.2 = (f32[2,32,40,256]{3,1,2,0:T(8,128)S(1)}, f32[2,32,40,256]{3,1,2,0:T(8,128)S(1)}, u32[]{:S(2)}, u32[]{:S(2)}) collective-permute-start(f32[2,32,40,256]{3,1,2,0:T(8,128)S(1)} %add.114), channel_id=1, source_target_pairs={{0,4},{1,5},{2,6},{3,7},{4,0},{5,1},{6,2},{7,3},{8,12},{9,13},{10,... | collective-permute-start | bytes 7864328 | tf_op jit(solution)/shard_map/ppermute | solution.py:102
  315.2 128.9 %collective-permute-start.3 = (f32[2,32,40,256]{3,1,2,0:T(8,128)S(1)}, f32[2,32,40,256]{3,1,2,0:T(8,128)S(1)}, u32[]{:S(2)}, u32[]{:S(2)}) collective-permute-start(f32[2,32,40,256]{3,1,2,0:T(8,128)S(1)} %add.115), channel_id=1, source_target_pairs={{0,8},{1,9},{2,10},{3,11},{4,12},{5,13},{6,14},{7,15},{8,0},{9,1},... | collective-permute-start | bytes 7864328 | tf_op jit(solution)/shard_map/ppermute | solution.py:102
  531.9 2.5 copy-start.1
